TPU v7x, 256 devices: a whole 4x4x8 slice. The times are simulated.
256 devices in a mesh: tsnk: 16 (over x, z_hi, core), tsrc: 16 (over y, z_lo).
Axes of the slice: x: 4, y: 4, z: 8 (z_hi: 2, z_lo: 4; z = z_hi * 4 + z_lo), core: 2. Of those that a mesh axis runs over, the one named last changes fastest.
Arguments:
- sink_vectors: bfloat16 [16, 2, 256, 3, 13824], P('tsnk', None, None, None, 'tsrc'), may hold values from -0.0546875 to 0.0546875
- source_vectors: bfloat16 [16, 2, 256, 3, 13824], P('tsrc', None, None, None, 'tsnk'), may hold values from -0.0546875 to 0.0546875
- peramb: bfloat16 [16, 16, 4, 2, 256, 4, 256], P('tsnk', 'tsrc'), may hold values from -6 to 6
- momenta: int32 [1, 3], replicated, may hold values from -3 to 3
- sink_times: int32 [16], P('tsnk'), may hold values from 0 to 255
- source_times: int32 [16], P('tsrc'), may hold values from 0 to 255
Outputs:
- correlator: float32 [1, 2, 16, 16], P(None, None, 'tsnk', 'tsrc')
All inputs are finite; a program needn't handle non-finite values.
Results may differ from a plain program's by a relative error of at most 0.0055.
Values may be sent and summed in bfloat16 or wider, within the bound.
A program may use at most 128 MiB of HBM per device.

v0:
```python
import math

import jax
import jax.numpy as jnp
from jax import lax
from jax.sharding import Mesh
from jax.sharding import PartitionSpec as P

VECS = 256
L = 24
MOM = 1
TSRC = ("tsrc_0", "tsrc_1")


GAMMA_FIVE = (1.0, 1.0, -1.0, -1.0)


def scatter_axes(value, axes, dim):
    if not axes:
        return value
    nearer = lax.psum_scatter(value, axes[0], scatter_dimension=dim, tiled=True)
    return scatter_axes(nearer, axes[1:], dim)


def cut_along(value, dim, peers):
    dims = value.shape
    tiles = value.reshape(*dims[:dim], peers, dims[dim] // peers, *dims[dim + 1 :])
    return jnp.moveaxis(tiles, dim, 0)


def sum_at_owner(value, axis, dim):
    tiles = cut_along(value, dim, lax.axis_size(axis))
    arrived = lax.all_to_all(tiles, axis, split_axis=0, concat_axis=0, tiled=True)
    return arrived.sum(axis=0)


def in_order(tiles, dim):
    tiles = jnp.moveaxis(tiles, 0, dim)
    dims = tiles.shape
    return tiles.reshape(*dims[:dim], dims[dim] * dims[dim + 1], *dims[dim + 2 :])


def from_everyone(value, axis):
    peers = lax.axis_size(axis)
    return lax.all_to_all(
        jnp.broadcast_to(value[None], (peers, *value.shape)), axis, 0, 0, tiled=True
    )


def gathered_copies(value, axis, dim):
    return in_order(from_everyone(value, axis), dim)


def partial_elemental(vectors, momenta, offset):
    count = vectors.shape[-1]
    site_index = offset + jnp.arange(count, dtype=jnp.int32)
    coord_x = site_index // (L * L)
    coord_y = site_index // L % L
    coord_z = site_index % L
    winding = (
        momenta[:, 0:1] * coord_x[None, :]
        + momenta[:, 1:2] * coord_y[None, :]
        + momenta[:, 2:3] * coord_z[None, :]
    ) % L
    angle = winding.astype(jnp.float32) * (2.0 * math.pi / L)
    cosine = jnp.cos(angle)
    sine = jnp.sin(angle)
    vec_real = vectors[0, 0]
    vec_imag = vectors[0, 1]
    left = jnp.concatenate([vec_real.reshape(VECS, -1), vec_imag.reshape(VECS, -1)], 1)
    blocks = []
    cos_m = cosine[0][None, None, :]
    sin_m = sine[0][None, None, :]
    wave_real = (cos_m * vec_real - sin_m * vec_imag).astype(jnp.bfloat16).reshape(VECS, -1)
    wave_imag = (cos_m * vec_imag + sin_m * vec_real).astype(jnp.bfloat16).reshape(VECS, -1)
    blocks.append(jnp.concatenate([wave_real, wave_imag], 1))
    blocks.append(jnp.concatenate([wave_imag, -wave_real], 1))
    right = jnp.concatenate(blocks, 0)
    return lax.dot_general(
        left, right, (((1,), (1,)), ((), ())), preferred_element_type=jnp.float32
    )


def correlate(sink_elem, source_elem, perm):
    spins = perm.shape[0]
    vecs = perm.shape[2]
    gamma_five = jnp.array(GAMMA_FIVE, dtype=jnp.float32)
    swapped = jnp.concatenate([perm[:, :, :, 2:], perm[:, :, :, :2]], 3)
    sink_real = sink_elem[:, 0, 0]
    sink_imag = sink_elem[:, 0, 1]
    src_real = source_elem[:, 0, 0]
    src_imag = source_elem[:, 0, 1]
    sink_stack = jnp.concatenate(
        [jnp.concatenate([sink_real, -sink_imag], 1), jnp.concatenate([sink_imag, sink_real], 1)], 0
    )
    source_stack = jnp.concatenate(
        [jnp.concatenate([src_real, src_imag], 1), jnp.concatenate([-src_imag, src_real], 1)], 0
    )
    total_real = jnp.zeros((), jnp.float32)
    total_imag = jnp.zeros((), jnp.float32)
    for spin_row in range(spins):
        left_spin = jnp.dot(
            sink_stack,
            perm[spin_row ^ 2].reshape(2 * vecs, spins * vecs),
            preferred_element_type=jnp.float32,
        ).reshape(2, vecs, spins, vecs)
        rows = jnp.moveaxis(swapped[spin_row], 0, 2).reshape(vecs * spins, 2 * vecs)
        right_spin = jnp.dot(rows, source_stack, preferred_element_type=jnp.float32).reshape(
            vecs, spins, 2, vecs
        )
        signs = (-gamma_five[spin_row] * gamma_five)[None, :, None]
        left_real = left_spin[0]
        left_imag = left_spin[1]
        right_real = right_spin[:, :, 0]
        right_imag = right_spin[:, :, 1]
        total_real = total_real + jnp.sum(signs * (left_real * right_real + left_imag * right_imag))
        total_imag = total_imag + jnp.sum(signs * (left_imag * right_real - left_real * right_imag))
    values = [jnp.stack([total_real, total_imag])]
    return jnp.stack(values)


def per_device(sink_vectors, source_vectors, peramb, momenta, sink_times, source_times):
    sink_count = sink_vectors.shape[-1]
    source_count = source_vectors.shape[-1]
    sink_terms = partial_elemental(sink_vectors, momenta, lax.axis_index(TSRC) * sink_count)
    source_terms = partial_elemental(source_vectors, momenta, lax.axis_index("tsnk") * source_count)
    sink_part = scatter_axes(sink_terms, TSRC, 0).astype(jnp.bfloat16)
    source_part = sum_at_owner(source_terms, "tsnk", 0).astype(jnp.bfloat16)
    sink_flat = gathered_copies(sink_part, TSRC, 0)
    source_flat = gathered_copies(source_part, "tsnk", 0)
    sink_elem = sink_flat.reshape(VECS, MOM, 2, VECS)
    source_elem = source_flat.reshape(VECS, MOM, 2, VECS)
    perm = peramb[0, 0]
    keep = sink_times[0] >= source_times[0]
    values = correlate(sink_elem, source_elem, perm) * keep.astype(jnp.float32)
    return values.reshape(MOM, 2, 1, 1)


def solution(mesh):
    split = Mesh(mesh.devices.reshape(mesh.shape["tsnk"], 4, 4), ("tsnk", "tsrc_0", "tsrc_1"))
    return jax.shard_map(
        per_device,
        mesh=split,
        in_specs=(
            P("tsnk", None, None, None, TSRC),
            P(TSRC, None, None, None, "tsnk"),
            P("tsnk", TSRC, None, None, None, None, None),
            P(),
            P("tsnk"),
            P(TSRC),
        ),
        out_specs=P(None, None, "tsnk", TSRC),
        check_vma=False,
    )
```

profile of v0, /device:TPU:4, one launch (start us, length us, event | category | flops | bytes accessed | tf_op | source)
XLA Modules:
  0.0 151.3 jit_solution(13483273639689272441)
XLA Ops:
  8.0 1.9 %fusion.75 = (f32[864]{0:T(1024)S(1)}, f32[864]{0:T(1024)S(1)}) fusion(s32[]{:T(128)} %bitcast.4, s32[]{:T(128)} %bitcast.3, s32[]{:T(128)S(6)} %mul.414, s32[]{:T(128)} %bitcast.2), kind=kLoop, calls=%fused_computation.121 | loop fusion | flops 32832 | bytes 6928 | tf_op jit(solution)/shard_map/sin | solution.py:67
  14.8 2.4 %fusion = f32[256,512]{1,0:T(8,128)} fusion(bf16[256,2592]{0,1:T(8,128)(2,1)S(1)} %get-tuple-element.19, bf16[256,2592]{0,1:T(8,128)(2,1)S(1)} %fusion.19, bf16[256,2592]{0,1:T(8,128)(2,1)S(1)} %get-tuple-element.20, bf16[256,2592]{0,1:T(8,128)(2,1)S(1)} %bitcast.117, bf16[256,2592]{0,1:T(8,128)(2,1)S(1)} %bitcast.116), kind=kOutput, calls=%fused_computation | convolution fusion | flops 1385496576 | bytes 7159808 | tf_op jit(solution)/shard_map/dot_general | solution.py:79
  17.2 1.9 %fusion.73 = (f32[864]{0:T(1024)S(1)}, f32[864]{0:T(1024)S(1)}) fusion(s32[]{:T(128)} %bitcast.4, s32[]{:T(128)} %bitcast.3, s32[]{:T(128)S(6)} %mul.433, s32[]{:T(128)} %bitcast.2), kind=kLoop, calls=%fused_computation.119 | loop fusion | flops 32832 | bytes 6928 | tf_op jit(solution)/shard_map/sin | solution.py:67
  22.3 2.4 %fusion.8 = f32[256,512]{1,0:T(8,128)} fusion(bf16[256,2592]{0,1:T(8,128)(2,1)S(1)} %get-tuple-element.23, bf16[256,2592]{0,1:T(8,128)(2,1)S(1)} %fusion.23, bf16[256,2592]{0,1:T(8,128)(2,1)S(1)} %get-tuple-element.24, bf16[256,2592]{0,1:T(8,128)(2,1)S(1)} %bitcast.119, bf16[256,2592]{0,1:T(8,128)(2,1)S(1)} %bitcast.118), kind=kOutput, calls=%fused_computation.8 | convolution fusion | flops 1385496576 | bytes 7159808 | tf_op jit(solution)/shard_map/dot_general | solution.py:79
  24.7 11.4 %all-to-all-start.1 = ((f32[16,16,512]{2,1,0:T(8,128)}), f32[16,16,512]{2,1,0:T(8,128)S(1)}, u32[]{:S(2)}, u32[]{:S(2)}) async-start(f32[16,16,512]{2,1,0:T(8,128)} %bitcast.11), calls=%async_computation.3 | async-start | bytes 1048576 | tf_op jit(solution)/shard_map/all_to_all | solution.py:33
  36.1 6.9 %fusion.90 = (bf16[4,2,256,2,256]{4,3,2,1,0:T(2,128)(2,1)S(1)}, bf16[4,2,256,2,256]{4,3,2,1,0:T(2,128)(2,1)S(1)}) fusion(bf16[4,2,256,4,256]{4,3,2,1,0:T(4,128)(2,1)} %bitcast.111), kind=kLoop, calls=%fused_computation.136 | loop fusion | bytes 8388608 | tf_op jit(solution)/shard_map/slice | solution.py:88
  43.0 5.2 %fusion.44 = (bf16[256,4,2,256]{3,1,0,2:T(4,128)(2,1)S(1)}, bf16[256,4,2,256]{3,1,0,2:T(4,128)(2,1)}, bf16[256,4,2,256]{3,1,0,2:T(4,128)(2,1)S(1)}, bf16[256,4,2,256]{3,1,0,2:T(4,128)(2,1)}) fusion(bf16[4,2,256,2,256]{4,3,2,1,0:T(2,128)(2,1)S(1)} %get-tuple-element.34, bf16[4,2,256,2,256]{4,3,2,1,0:T(2,128)(2,1)S(1)} %get-tuple-element.33), kind=kLoop, calls=%fused_computation.67 | loop fusion | flops 8388608 | bytes 8388608 | tf_op jit(solution)/shard_map/transpose | solution.py:107
  50.3 8.4 %all-to-all-start.2 = ((bf16[16,16,512]{2,1,0:T(8,128)(2,1)}), bf16[16,16,512]{2,1,0:T(8,128)(2,1)S(1)}, u32[]{:S(2)}, u32[]{:S(2)}) async-start(bf16[16,16,512]{2,1,0:T(8,128)(2,1)} %broadcast_in_dim.5), calls=%async_computation.4 | async-start | bytes 524288 | tf_op jit(solution)/shard_map/all_to_all | solution.py:45
  58.9 4.0 %fusion.89 = (bf16[1,1,1,2,256,4,256]{6,5,4,3,2,1,0:T(4,128)(2,1)}, bf16[1,1,1,2,256,4,256]{6,5,4,3,2,1,0:T(4,128)(2,1)S(1)}, bf16[1,1,1,2,256,4,256]{6,5,4,3,2,...) fusion(bf16[1,1,4,2,256,4,256]{6,5,4,3,2,1,0:T(4,128)(2,1)} %param.9), kind=kLoop, calls=%fused_computation.135 | loop fusion | bytes 8388608 | tf_op jit(solution)/shard_map/slice | solution.py:104
  63.0 2.5 %copy.78 = bf16[64,8,4,256]{3,1,2,0:T(8,128)(2,1)} copy(bf16[64,8,4,256]{3,2,1,0:T(4,128)(2,1)} %bitcast.131) | data formatting | bytes 2097152
  71.1 2.5 %copy.81 = bf16[64,8,4,256]{3,1,2,0:T(8,128)(2,1)} copy(bf16[64,8,4,256]{3,2,1,0:T(4,128)(2,1)} %bitcast.129) | data formatting | bytes 2097152
  77.5 2.3 %copy.58 = bf16[256,4,2,256]{3,2,0,1:T(2,128)(2,1)S(1)} copy(bf16[256,4,2,256]{3,1,0,2:T(4,128)(2,1)} %get-tuple-element.32) | data formatting | bytes 2097152 | tf_op jit(solution)/shard_map/transpose | solution.py:107
  81.9 8.6 %reduce-scatter.5.cloned.1.call-done = f32[16,512]{1,0:T(8,128)} async-done(((f32[64,512]{1,0:T(8,128)}), f32[16,512]{1,0:T(8,128)}) %reduce-scatter.5.cloned.1.call-update) | async-done | bytes 32784 | tf_op jit(solution)/shard_map/reduce_scatter | solution.py:21
  92.0 4.5 %all-to-all-start = ((bf16[16,16,512]{2,1,0:T(8,128)(2,1)}), bf16[16,16,512]{2,1,0:T(8,128)(2,1)}, u32[]{:S(2)}, u32[]{:S(2)}) async-start(bf16[16,16,512]{2,1,0:T(8,128)(2,1)} %broadcast_in_dim.4), calls=%async_computation.2 | async-start | bytes 524288 | tf_op jit(solution)/shard_map/all_to_all | solution.py:45
  97.2 2.0 %fusion.40 = f32[256,4,2,256]{0,3,2,1:T(8,128)S(1)} fusion(bf16[2,256,512,1]{2,1,0,3:T(8,128)(2,1)S(1)} %bitcast.112, bf16[256,4,512,1]{2,0,1,3:T(8,128)(2,1)} %reshape.279), kind=kOutput, calls=%fused_computation.55 | convolution fusion | flops 536870912 | bytes 3670016 | tf_op jit(solution)/shard_map/dot_general | solution.py:108
  100.7 2.5 %copy.65 = f32[256,1024]{1,0:T(8,128)} copy(f32[256,1024]{0,1:T(8,128)} %bitcast.124) | data formatting | bytes 2097152 | tf_op jit(solution)/shard_map/squeeze | solution.py:114
  103.3 2.6 %copy.66 = f32[256,1024]{1,0:T(8,128)} copy(f32[256,1024]{0,1:T(8,128)} %bitcast.120) | data formatting | bytes 2097152 | tf_op jit(solution)/shard_map/squeeze | solution.py:115
  108.1 2.7 %copy.67 = f32[256,1024]{1,0:T(8,128)} copy(f32[256,1024]{0,1:T(8,128)} %bitcast.125) | data formatting | bytes 2097152 | tf_op jit(solution)/shard_map/squeeze | solution.py:114
  110.8 2.5 %copy.68 = f32[256,1024]{1,0:T(8,128)} copy(f32[256,1024]{0,1:T(8,128)} %bitcast.121) | data formatting | bytes 2097152 | tf_op jit(solution)/shard_map/squeeze | solution.py:115
  117.1 2.6 %copy.70 = f32[256,1024]{1,0:T(8,128)} copy(f32[256,1024]{0,1:T(8,128)} %bitcast.122) | data formatting | bytes 2097152 | tf_op jit(solution)/shard_map/squeeze | solution.py:115
  128.2 2.1 %fusion.80 = f32[512,1024]{1,0:T(8,128)} fusion(bf16[512,1024]{1,0:T(8,128)(2,1)S(1)} %bitcast.134, bf16[256,256]{1,0:T(8,128)(2,1)S(1)} %bitcast.139, bf16[256,256]{1,0:T(8,128)(2,1)S(1)} %get-tuple-element.18, bf16[256,256]{1,0:T(8,128)(2,1)S(1)} %get-tuple-element.17), kind=kOutput, calls=%fused_computation.128 | convolution fusion | flops 538968064 | bytes 3538944 | tf_op jit(solution)/shard_map/dot_general | solution.py:102
  130.2 2.0 %fusion.79 = f32[512,1024]{1,0:T(8,128)} fusion(bf16[512,1024]{1,0:T(8,128)(2,1)S(1)} %bitcast.135, bf16[256,256]{1,0:T(8,128)(2,1)S(1)} %bitcast.140, bf16[256,256]{1,0:T(8,128)(2,1)S(1)} %get-tuple-element.18, bf16[256,256]{1,0:T(8,128)(2,1)S(1)} %get-tuple-element.17), kind=kOutput, calls=%fused_computation.127 | convolution fusion | flops 538968064 | bytes 3538944 | tf_op jit(solution)/shard_map/dot_general | solution.py:102
  132.6 2.1 %multiply_reduce_fusion.6 = (f32[]{:T(128)}, f32[]{:T(128)}, f32[]{:T(128)}, f32[]{:T(128)}) fusion(f32[256,1024]{1,0:T(8,128)S(1)} %copy-done.5, f32[256,1024]{1,0:T(8,128)S(1)} %copy-done.3, f32[512,1024]{1,0:T(8,128)S(1)} %fusion.81, f32[1024]{0:T(1024)S(1)} %bitcast.141, f32[256,1024]{1,0:T(8,128)S(1)} %copy-done.2, f32[512,1024]{1,0:T(8,128)S(1)} %fusion.82, ...), kind=kLoop, calls=%fused_computation.63 | loop fusion | flops 5242876 | bytes 8392720 | tf_op jit(solution)/shard_map/reduce_sum | solution.py:116
  136.0 4.1 %multiply_reduce_fusion.4 = (f32[]{:T(128)}, f32[]{:T(128)}, f32[]{:T(128)}, f32[]{:T(128)}) fusion(f32[256,1024]{1,0:T(8,128)} %copy.72, f32[256,1024]{1,0:T(8,128)S(1)} %copy.71, f32[512,1024]{1,0:T(8,128)} %fusion.79, f32[1024]{0:T(1024)S(1)} %bitcast.142, f32[256,1024]{1,0:T(8,128)S(1)} %copy-done.4, f32[512,1024]{1,0:T(8,128)} %fusion.80, ...), kind=kLoop, calls=%fused_computation.61 | loop fusion | flops 5242876 | bytes 8392720 | tf_op jit(solution)/shard_map/reduce_sum | solution.py:116
  (93 shorter events, 41.1 us)
Async XLA Ops:
  6.5 56.3 %reduce-scatter.3.cloned.1.call-start = ((), (), s32[]{:S(2)}) async-start(), calls=%async_computation.5 | async-start | bytes 655360 | tf_op jit(solution)/shard_map/reduce_scatter | solution.py:21
  14.7 4.5 %copy-start.8 = (bf16[1,2,256,3,864]{2,4,3,1,0:T(8,128)(2,1)S(1)}, bf16[1,2,256,3,864]{2,4,3,1,0:T(8,128)(2,1)}, u32[]{:S(2)}) copy-start(bf16[1,2,256,3,864]{2,4,3,1,0:T(8,128)(2,1)} %param.8) | copy-start | bytes 7962628
  24.7 24.8 %all-to-all-start.1 = ((f32[16,16,512]{2,1,0:T(8,128)}), f32[16,16,512]{2,1,0:T(8,128)S(1)}, u32[]{:S(2)}, u32[]{:S(2)}) async-start(f32[16,16,512]{2,1,0:T(8,128)} %bitcast.11), calls=%async_computation.3 | async-start | bytes 1048576 | tf_op jit(solution)/shard_map/all_to_all | solution.py:33
  50.3 41.0 %all-to-all-start.2 = ((bf16[16,16,512]{2,1,0:T(8,128)(2,1)}), bf16[16,16,512]{2,1,0:T(8,128)(2,1)S(1)}, u32[]{:S(2)}, u32[]{:S(2)}) async-start(bf16[16,16,512]{2,1,0:T(8,128)(2,1)} %broadcast_in_dim.5), calls=%async_computation.4 | async-start | bytes 524288 | tf_op jit(solution)/shard_map/all_to_all | solution.py:45
  58.6 4.2 %copy-start.14 = (f32[4]{0:T(128)S(1)}, f32[4]{0:T(128)}, u32[]{:S(2)}) copy-start(f32[4]{0:T(128)} %constant.81) | copy-start | bytes 52
  58.6 31.8 %reduce-scatter.5.cloned.1.call-start = ((), (), s32[]{:S(2)}) async-start(), calls=%async_computation.6 | async-start | bytes 163840 | tf_op jit(solution)/shard_map/reduce_scatter | solution.py:21
  63.0 3.8 %copy-start.6 = (bf16[256,4,2,256]{3,1,0,2:T(4,128)(2,1)S(1)}, bf16[256,4,2,256]{3,1,0,2:T(4,128)(2,1)}, u32[]{:S(2)}) copy-start(bf16[256,4,2,256]{3,1,0,2:T(4,128)(2,1)} %get-tuple-element.30) | copy-start | bytes 3145732
  71.1 2.5 %copy-start.7 = (bf16[1,1,1,2,256,4,256]{6,5,4,3,2,1,0:T(4,128)(2,1)S(1)}, bf16[1,1,1,2,256,4,256]{6,5,4,3,2,1,0:T(4,128)(2,1)}, u32[]{:S(2)}) copy-start(bf16[1,1,1,2,256,4,256]{6,5,4,3,2,1,0:T(4,128)(2,1)} %get-tuple-element.28) | copy-start | bytes 3145732
  77.5 3.0 %copy-start.13 = (f32[4]{0:T(128)S(1)}, f32[4]{0:T(128)}, u32[]{:S(2)}) copy-start(f32[4]{0:T(128)} %constant.89) | copy-start | bytes 52
  92.0 32.6 %all-to-all-start = ((bf16[16,16,512]{2,1,0:T(8,128)(2,1)}), bf16[16,16,512]{2,1,0:T(8,128)(2,1)}, u32[]{:S(2)}, u32[]{:S(2)}) async-start(bf16[16,16,512]{2,1,0:T(8,128)(2,1)} %broadcast_in_dim.4), calls=%async_computation.2 | async-start | bytes 524288 | tf_op jit(solution)/shard_map/all_to_all | solution.py:45
  108.1 5.2 %copy-start = (bf16[256,4,512,1]{2,0,1,3:T(8,128)(2,1)S(1)}, bf16[256,4,512,1]{2,0,1,3:T(8,128)(2,1)}, u32[]{:S(2)}) copy-start(bf16[256,4,512,1]{2,0,1,3:T(8,128)(2,1)} %reshape.282) | copy-start | bytes 3145732
  124.6 1.6 %copy-start.9 = (bf16[64,8,4,256]{3,1,2,0:T(8,128)(2,1)S(1)}, bf16[64,8,4,256]{3,1,2,0:T(8,128)(2,1)}, u32[]{:S(2)}) copy-start(bf16[64,8,4,256]{3,1,2,0:T(8,128)(2,1)} %copy.78) | copy-start | bytes 3145732
  126.1 1.2 copy-start.10
  126.9 1.3 copy-start.11
  128.0 2.2 %copy-start.12 = (bf16[64,8,4,256]{3,1,2,0:T(8,128)(2,1)S(1)}, bf16[64,8,4,256]{3,1,2,0:T(8,128)(2,1)}, u32[]{:S(2)}) copy-start(bf16[64,8,4,256]{3,1,2,0:T(8,128)(2,1)} %copy.82) | copy-start | bytes 3145732
  128.2 4.1 %copy-start.5 = (f32[256,1024]{1,0:T(8,128)S(1)}, f32[256,1024]{1,0:T(8,128)}, u32[]{:S(2)}) copy-start(f32[256,1024]{1,0:T(8,128)} %copy.68) | copy-start | bytes 3145732
  130.2 2.1 %copy-start.1 = (f32[256,1024]{1,0:T(8,128)S(1)}, f32[256,1024]{1,0:T(8,128)}, u32[]{:S(2)}) copy-start(f32[256,1024]{1,0:T(8,128)} %copy.65) | copy-start | bytes 3145732
  130.2 2.1 %copy-start.2 = (f32[256,1024]{1,0:T(8,128)S(1)}, f32[256,1024]{1,0:T(8,128)}, u32[]{:S(2)}) copy-start(f32[256,1024]{1,0:T(8,128)} %copy.66) | copy-start | bytes 3145732
  130.2 2.3 %copy-start.3 = (f32[256,1024]{1,0:T(8,128)S(1)}, f32[256,1024]{1,0:T(8,128)}, u32[]{:S(2)}) copy-start(f32[256,1024]{1,0:T(8,128)} %copy.67) | copy-start | bytes 3145732
  132.6 3.4 %copy-start.4 = (f32[256,1024]{1,0:T(8,128)S(1)}, f32[256,1024]{1,0:T(8,128)}, u32[]{:S(2)}) copy-start(f32[256,1024]{1,0:T(8,128)} %copy.70) | copy-start | bytes 3145732
Sparse Core Ops, SparseCore 0:
  17.3 27.1 reduce-scatter.2
  63.0 27.4 reduce-scatter.4
where the time goes:
time: 153 us; the launch traced here: 151 us
  local copies, waits for them, and re-layouts  60 us (39%)
  starting transfers between devices  24.5 us (16%)
  other arithmetic  22.4 us (15%)
  between operations  20 us (13%)
  matrix products  14.5 us (9%)
  waiting for transfers between devices  9.92 us (6%)
    all_to_all x2, starting transfers between devices, from_everyone(): lax.all_to_all(jnp.broadcast_to(value[None], (peers, *value.shape)), axis...  12.8 us
    all_to_all x1, starting transfers between devices, sum_at_owner(): lax.all_to_all(tiles, axis, split_axis=0, concat_axis=0, tiled=True)  11.4 us
    squeeze x4, local copies, waits for them, and re-layouts, correlate(): right_imag = right_spin[:, :, 1]  9.08 us
    reduce_scatter x2, waiting for transfers between devices, scatter_axes(): nearer = lax.psum_scatter(value, axes[0], scatter_dimension=dim, tiled=True)  8.6 us
    unnamed x40, local copies, waits for them, and re-layouts  8.58 us
    squeeze x4, local copies, waits for them, and re-layouts, correlate(): right_real = right_spin[:, :, 0]  8.3 us
    slice x1, local copies, waits for them, and re-layouts, correlate(): swapped = jnp.concatenate([perm[:, :, :, 2:], perm[:, :, :, :2]], 3)  6.88 us
    reduce_sum x2, other arithmetic, correlate(): jnp.sum(signs * (left_real * right_real + left_imag * right_imag))  6.28 us
  transfers between devices with their start and end apart: 5, of which 2 were waited for; matrix products, arithmetic and copies ran while one was open for 47% of the time, Pallas kernels for 0%

commit v1 on v0

v1 whole, which is shorter than its diff:
```python
import math

import jax
import jax.numpy as jnp
from jax import lax
from jax.experimental import pallas as pl
from jax.experimental.pallas import tpu as pltpu
from jax.sharding import PartitionSpec as P

VECS = 256
L = 24
SITES = 864
COLOURS = 3
MESH = pl.DeviceIdType.MESH
COS = [math.cos(2.0 * math.pi * k / L) for k in range(L)]
SIN = [math.sin(2.0 * math.pi * k / L) for k in range(L)]


def mod_winding(v):
    return v - 24.0 * jnp.floor((v + 0.5) * (1.0 / 24.0))


def cos_sin(k):
    cosine = jnp.zeros_like(k)
    sine = jnp.zeros_like(k)
    for m in range(L):
        hit = k == float(m)
        cosine = jnp.where(hit, COS[m], cosine)
        sine = jnp.where(hit, SIN[m], sine)
    return cosine, sine


def phase_tables(mom_ref, first_row, cos_ref, sin_ref):
    px = mom_ref[0, 0].astype(jnp.float32)
    py = mom_ref[0, 1].astype(jnp.float32)
    pz = mom_ref[0, 2].astype(jnp.float32)
    z = lax.broadcasted_iota(jnp.int32, (L, 128), 0).astype(jnp.float32)
    cos_z, sin_z = cos_sin(mod_winding(pz * z))
    row = (lax.broadcasted_iota(jnp.int32, (40, 128), 0) + first_row).astype(jnp.float32)
    x = jnp.floor((row + 0.5) * (1.0 / L))
    y = row - L * x
    cos_q, sin_q = cos_sin(mod_winding(px * x + py * y))
    for q in range(SITES // L):
        cq = jnp.broadcast_to(cos_q[q : q + 1, :], (L, 128))
        sq = jnp.broadcast_to(sin_q[q : q + 1, :], (L, 128))
        cos_ref[q * L : (q + 1) * L, :] = cq * cos_z - sq * sin_z
        sin_ref[q * L : (q + 1) * L, :] = sq * cos_z + cq * sin_z


def partial_elemental(colour_copies, vec_ref, wave_ref, cos_ref, sin_ref, acc_ref, out_ref):
    rows = 96
    for colour in range(COLOURS):
        for copy in colour_copies[colour]:
            copy.wait()

        def block(step, carry):
            at = pl.ds(pl.multiple_of(step * rows, rows), rows)
            cosine = cos_ref[at, :]
            sine = sin_ref[at, :]
            for half in range(2):
                lanes = pl.ds(half * 128, 128)
                lanes_imag = pl.ds(256 + half * 128, 128)
                real = vec_ref[colour, at, lanes].astype(jnp.float32)
                imag = vec_ref[colour, at, lanes_imag].astype(jnp.float32)
                wave_ref[colour, at, lanes] = (cosine * real - sine * imag).astype(jnp.bfloat16)
                wave_ref[colour, at, lanes_imag] = (cosine * imag + sine * real).astype(jnp.bfloat16)
            return carry

        lax.fori_loop(0, SITES // rows, block, 0)
        term = lax.dot_general(
            vec_ref[colour], wave_ref[colour], (((0,), (0,)), ((), ())), preferred_element_type=jnp.float32
        )
        if colour == 0:
            acc_ref[...] = term
        elif colour < COLOURS - 1:
            acc_ref[...] += term
        else:
            term = term + acc_ref[...]
            out_ref[:, 0:256] = term[0:256, 0:256] + term[256:512, 256:512]
            out_ref[:, 256:512] = term[0:256, 256:512] - term[256:512, 0:256]


def kernel(
    sink_hbm, source_hbm, per_hbm, mom_ref, snk_t, src_t,
    out_ref,
    snk_vec, src_vec, wave, cos_ref, sin_ref, acc,
    snk_part, src_part, per, pt, tbuf,
    y_recv, y_sum, z_recv, elem, core_recv, core_sum, x_recv, x_sum, zz_recv, src_elem,
    est, sst, tot,
    load_sem, send_sem, recv_sem,
):
    i = lax.axis_index("tsnk")
    j = lax.axis_index("tsrc")
    x, zh, c = i // 4, (i // 2) % 2, i % 2
    y, zl = j // 4, j % 4
    core_peer = (4 * x + 2 * zh + (1 - c), j)
    z_peer = (4 * x + 2 * (1 - zh) + c, j)
    x_peers = [(4 * ((x + d) % 4) + 2 * zh + c, j) for d in (1, 2, 3)]
    y_peers = [(i, 4 * ((y + d) % 4) + zl) for d in (1, 2, 3)]
    zl_peers = [(i, 4 * y + (zl + d) % 4) for d in (1, 2, 3)]

    def load(n, src, dst):
        copy = pltpu.make_async_copy(src, dst, load_sem.at[n])
        copy.start()
        return copy

    snk_loads = [
        [load(2 * k + r, sink_hbm.at[r, k], snk_vec.at[k, :, pl.ds(r * 256, 256)]) for r in range(2)]
        for k in range(COLOURS)
    ]
    src_loads = [
        [load(6 + 2 * k + r, source_hbm.at[r, k], src_vec.at[k, :, pl.ds(r * 256, 256)]) for r in range(2)]
        for k in range(COLOURS)
    ]
    per_loads = [load(12 + s, per_hbm.at[s], per.at[s]) for s in range(4)]

    barrier = pltpu.get_barrier_semaphore()
    peers = [core_peer, z_peer] + x_peers + y_peers + zl_peers
    for peer in peers:
        pl.semaphore_signal(barrier, inc=1, device_id=peer, device_id_type=MESH)

    def remote(n, src, dst, peer):
        return pltpu.make_async_remote_copy(
            src_ref=src, dst_ref=dst, send_sem=send_sem.at[n], recv_sem=recv_sem.at[n],
            device_id=peer, device_id_type=MESH,
        )

    def start(copies):
        for copy in copies:
            copy.start()

    phase_tables(mom_ref, j * (SITES // L), cos_ref, sin_ref)
    partial_elemental(snk_loads, snk_vec, wave, cos_ref, sin_ref, acc, snk_part)
    pl.semaphore_wait(barrier, len(peers))
    sent = []

    def block_of(start_row, size):
        return pl.ds(pl.multiple_of(start_row, size), size)

    y_rs = [
        remote(d, snk_part.at[block_of(64 * ((y + d + 1) % 4), 64)], y_recv.at[d], y_peers[d]) for d in range(3)
    ]
    start(y_rs)

    phase_tables(mom_ref, i * (SITES // L), cos_ref, sin_ref)
    partial_elemental(src_loads, src_vec, wave, cos_ref, sin_ref, acc, src_part)
    core_rs = remote(3, src_part.at[block_of(128 * (1 - c), 128)], core_recv, core_peer)
    core_rs.start()

    out_row = lax.broadcasted_iota(jnp.int32, (256, 256), 0)
    in_row = lax.broadcasted_iota(jnp.int32, (256, 256), 1)
    pick = jnp.where((out_row % 32) * 8 + out_row // 32 == in_row, 1.0, 0.0).astype(jnp.bfloat16)

    def unmix(s, carry):
        per_loads_wait = pltpu.make_async_copy(per_hbm.at[s], per.at[s], load_sem.at[12 + s])
        per_loads_wait.wait()
        for blk in range(8):
            rows = pl.ds(blk * 256, 256)
            both = jnp.concatenate([per[s, 0, rows, :], per[s, 1, rows, :]], axis=1)
            moved = jnp.dot(pick, both, preferred_element_type=jnp.float32).astype(jnp.bfloat16)
            for t in range(4):
                for half in range(2):
                    piece = moved[(half * 4 + t) * 32 : (half * 4 + t + 1) * 32, :]
                    for r in range(2):
                        pt[s, t, pl.ds(blk * 32, 32), pl.ds(r * 256 + half * 128, 128)] = piece[
                            :, r * 128 : (r + 1) * 128
                        ]
        return carry

    lax.fori_loop(0, 2, unmix, 0)
    core_rs.wait_recv()
    core_sum[...] = src_part[block_of(128 * c, 128), :] + core_recv[...]
    x_rs = [
        remote(4 + d, core_sum.at[block_of(32 * ((x + d + 1) % 4), 32)], x_recv.at[d], x_peers[d]) for d in range(3)
    ]
    start(x_rs)
    lax.fori_loop(2, 4, unmix, 0)

    for copy in y_rs:
        copy.wait_recv()
    y_sum[...] = (snk_part[block_of(64 * y, 64), :] + y_recv[0]) + (y_recv[1] + y_recv[2])
    z_rs = [
        remote(7 + d, y_sum.at[block_of(16 * ((zl + d + 1) % 4), 16)], z_recv.at[d], zl_peers[d]) for d in range(3)
    ]
    start(z_rs)

    for copy in x_rs:
        copy.wait_recv()
    x_sum[...] = (core_sum[block_of(32 * x, 32), :] + x_recv[0]) + (x_recv[1] + x_recv[2])
    zz = remote(10, x_sum, zz_recv, z_peer)
    zz.start()

    for copy in z_rs:
        copy.wait_recv()
    mine = (y_sum[block_of(16 * zl, 16), :] + z_recv[0]) + (z_recv[1] + z_recv[2])
    own = elem.at[block_of(64 * y + 16 * zl, 16)]
    own[...] = mine.astype(jnp.bfloat16)
    z_ag = [remote(11 + d, own, own, zl_peers[d]) for d in range(3)]
    start(z_ag)
    y_ag = [remote(14 + d, own, own, y_peers[d]) for d in range(3)]
    start(y_ag)

    zz.wait_recv()
    src_own = src_elem.at[block_of(128 * c + 32 * x, 32)]
    src_own[...] = (x_sum[...] + zz_recv[...]).astype(jnp.bfloat16)
    x_ag = [remote(26 + d, src_own, src_own, x_peers[d]) for d in range(3)]
    start(x_ag)
    core_ag = [remote(29, src_own, src_own, core_peer)]
    start(core_ag)

    for d in range(3):
        z_ag[d].wait_recv()
        came = elem.at[block_of(64 * y + 16 * ((zl + 3 - d) % 4), 16)]
        onward = [remote(17 + 3 * d + e, came, came, y_peers[e]) for e in range(3)]
        start(onward)
        y_ag += onward
    for d in range(3):
        x_ag[d].wait_recv()
        came = src_elem.at[block_of(128 * c + 32 * ((x + 3 - d) % 4), 32)]
        onward = remote(30 + d, came, came, core_peer)
        onward.start()
        core_ag.append(onward)
    for copy in core_ag:
        copy.wait_recv()

    sst[0:256, :] = src_elem[...]
    sst[256:512, 0:256] = -src_elem[:, 256:512]
    sst[256:512, 256:512] = src_elem[:, 0:256]

    def right(s, carry):
        for t in range(4):
            tbuf[s, t] = jnp.dot(pt[s, t], sst[...], preferred_element_type=jnp.float32)
        return carry

    lax.fori_loop(0, 4, right, 0)

    for copy in y_ag:
        copy.wait_recv()
    est[0:256, 0:256] = elem[:, 0:256]
    est[0:256, 256:512] = -elem[:, 256:512]
    est[256:512, 0:256] = elem[:, 256:512]
    est[256:512, 256:512] = elem[:, 0:256]
    tot[...] = jnp.zeros_like(tot)

    def fold(v):
        return v.reshape(32, 8, 256).sum(axis=0)

    def left(s, carry):
        other = (s + 2) % 4
        sum_real = jnp.zeros((8, 256), jnp.float32)
        sum_imag = jnp.zeros((8, 256), jnp.float32)
        for t in range(4):
            lt = jnp.dot(est[:, 0:256], pt[s, t, :, 0:256], preferred_element_type=jnp.float32)
            lt = lt + jnp.dot(est[:, 256:512], pt[s, t, :, 256:512], preferred_element_type=jnp.float32)
            right_real = tbuf[other, t ^ 2, :, 0:256]
            right_imag = tbuf[other, t ^ 2, :, 256:512]
            left_real = lt[0:256]
            left_imag = lt[256:512]
            real = fold(left_real * right_real + left_imag * right_imag)
            imag = fold(left_imag * right_real - left_real * right_imag)
            if t < 2:
                sum_real, sum_imag = sum_real + real, sum_imag + imag
            else:
                sum_real, sum_imag = sum_real - real, sum_imag - imag
        sign = 1.0 - 2.0 * (s // 2).astype(jnp.float32)
        tot[0] += sign * sum_real
        tot[1] += sign * sum_imag
        return carry

    lax.fori_loop(0, 4, left, 0)
    keep = jnp.where(snk_t[0] >= src_t[0], 1.0, 0.0)
    out_ref[0, 0] = jnp.sum(tot[0]) * keep
    out_ref[0, 1] = jnp.sum(tot[1]) * keep

    for copy in y_rs + [core_rs] + x_rs + z_rs + [zz] + z_ag + y_ag + x_ag + core_ag:
        copy.wait_send()


def per_device(sink_vectors, source_vectors, peramb, momenta, sink_times, source_times):
    sink = sink_vectors[0].transpose(0, 2, 3, 1)
    source = source_vectors[0].transpose(0, 2, 3, 1)
    per = peramb[0, 0].reshape(4, 2, 256, 4, 2, 128).transpose(0, 1, 2, 4, 3, 5).reshape(4, 2, 2048, 128)
    hbm = pl.BlockSpec(memory_space=pl.ANY)
    smem = pl.BlockSpec(memory_space=pltpu.SMEM)
    f32, bf16 = jnp.float32, jnp.bfloat16
    values = pl.pallas_call(
        kernel,
        out_shape=jax.ShapeDtypeStruct((1, 2), f32),
        in_specs=[hbm, hbm, hbm, smem, smem, smem],
        out_specs=smem,
        scratch_shapes=[
            pltpu.VMEM((COLOURS, SITES, 512), bf16),
            pltpu.VMEM((COLOURS, SITES, 512), bf16),
            pltpu.VMEM((COLOURS, SITES, 512), bf16),
            pltpu.VMEM((SITES, 128), f32),
            pltpu.VMEM((SITES, 128), f32),
            pltpu.VMEM((512, 512), f32),
            pltpu.VMEM((256, 512), f32),
            pltpu.VMEM((256, 512), f32),
            pltpu.VMEM((4, 2, 2048, 128), bf16),
            pltpu.VMEM((4, 4, 256, 512), bf16),
            pltpu.VMEM((4, 4, 256, 512), f32),
            pltpu.VMEM((3, 64, 512), f32),
            pltpu.VMEM((64, 512), f32),
            pltpu.VMEM((3, 16, 512), f32),
            pltpu.VMEM((256, 512), bf16),
            pltpu.VMEM((128, 512), f32),
            pltpu.VMEM((128, 512), f32),
            pltpu.VMEM((3, 32, 512), f32),
            pltpu.VMEM((32, 512), f32),
            pltpu.VMEM((32, 512), f32),
            pltpu.VMEM((256, 512), bf16),
            pltpu.VMEM((512, 512), bf16),
            pltpu.VMEM((512, 512), bf16),
            pltpu.VMEM((2, 8, 256), f32),
            pltpu.SemaphoreType.DMA((16,)),
            pltpu.SemaphoreType.DMA((33,)),
            pltpu.SemaphoreType.DMA((33,)),
        ],
        compiler_params=pltpu.CompilerParams(
            collective_id=0, has_side_effects=True, vmem_limit_bytes=60 * 1024 * 1024
        ),
    )(sink, source, per, momenta, sink_times, source_times)
    return values.reshape(1, 2, 1, 1)


def solution(mesh):
    return jax.shard_map(
        per_device,
        mesh=mesh,
        in_specs=(
            P("tsnk", None, None, None, "tsrc"),
            P("tsrc", None, None, None, "tsnk"),
            P("tsnk", "tsrc", None, None, None, None, None),
            P(),
            P("tsnk"),
            P("tsrc"),
        ),
        out_specs=P(None, None, "tsnk", "tsrc"),
        check_vma=False,
    )
```

time: 153 us -> 46.7 us (0.31)
  the two profiles are of different devices: /device:TPU:4 before, /device:TPU:1 now
where the time goes in v1:
time: 46.7 us; the launch traced here: 46.6 us
  Pallas kernels  44.1 us (94%)
  between operations  1.3 us (3%)
  local copies, waits for them, and re-layouts  1.19 us (3%)
    pallas_call x1, Pallas kernels, per_device(): pl.pallas_call(kernel, out_shape=jax.ShapeDtypeStruct((1, 2), f32), in_sp...  44.1 us
    unnamed x1, local copies, waits for them, and re-layouts  1.19 us

profile of v1, /device:TPU:1, one launch (start us, length us, event | category | flops | bytes accessed | tf_op | source)
XLA Modules:
  0.0 46.6 jit_solution(4274472458311840512)
XLA Ops:
  1.3 44.1 %shard_map.64 = f32[1,2]{1,0:T(1,128)} custom-call(bf16[2,3,864,256]{3,2,1,0:T(8,128)(2,1)} %bitcast.13, bf16[2,3,864,256]{3,2,1,0:T(8,128)(2,1)} %bitcast.14, bf16[4,2,2048,128]{3,2,1,0:T(8,128)(2,1)} %bitcast.12, s32[1,3]{1,0:T(1,128)} %mom_ref.1, s32[1]{0:T(128)S(6)} %copy.9.snk_t, s32[1]{0:T(128)S(6)} %copy.10.src_t), custom_call_target="tpu_custom_call" | custom-call | tf_op jit(solution)/shard_map/pallas_call | solution.py:286
  45.4 1.2 %copy.11 = f32[1,2,1,1]{1,3,2,0:T(1,128)} copy(f32[1,2,1,1]{1,3,2,0:T(1,128)} %bitcast.15) | data formatting | bytes 16

commit v2 on v1

--- a/solution.py
+++ b/solution.py
@@ -47,43 +47,36 @@
         sin_ref[q * L : (q + 1) * L, :] = sq * cos_z + cq * sin_z
 
 
-def partial_elemental(colour_copies, vec_ref, wave_ref, cos_ref, sin_ref, acc_ref, out_ref):
-    rows = 96
-    for colour in range(COLOURS):
-        for copy in colour_copies[colour]:
-            copy.wait()
-
-        def block(step, carry):
-            at = pl.ds(pl.multiple_of(step * rows, rows), rows)
-            cosine = cos_ref[at, :]
-            sine = sin_ref[at, :]
-            for half in range(2):
-                lanes = pl.ds(half * 128, 128)
-                lanes_imag = pl.ds(256 + half * 128, 128)
-                real = vec_ref[colour, at, lanes].astype(jnp.float32)
-                imag = vec_ref[colour, at, lanes_imag].astype(jnp.float32)
-                wave_ref[colour, at, lanes] = (cosine * real - sine * imag).astype(jnp.bfloat16)
-                wave_ref[colour, at, lanes_imag] = (cosine * imag + sine * real).astype(jnp.bfloat16)
-            return carry
-
-        lax.fori_loop(0, SITES // rows, block, 0)
-        term = lax.dot_general(
-            vec_ref[colour], wave_ref[colour], (((0,), (0,)), ((), ())), preferred_element_type=jnp.float32
-        )
-        if colour == 0:
-            acc_ref[...] = term
-        elif colour < COLOURS - 1:
-            acc_ref[...] += term
-        else:
-            term = term + acc_ref[...]
-            out_ref[:, 0:256] = term[0:256, 0:256] + term[256:512, 256:512]
-            out_ref[:, 256:512] = term[0:256, 256:512] - term[256:512, 0:256]
+def wave_of(colour, vec_ref, wave_ref, cos_ref, sin_ref):
+    rows = 48
+    for step in range(SITES // rows):
+        at = pl.ds(step * rows, rows)
+        cosine = cos_ref[at, :]
+        sine = sin_ref[at, :]
+        for half in range(2):
+            lanes = pl.ds(half * 128, 128)
+            lanes_imag = pl.ds(256 + half * 128, 128)
+            real = vec_ref[colour, at, lanes].astype(jnp.float32)
+            imag = vec_ref[colour, at, lanes_imag].astype(jnp.float32)
+            wave_ref[colour, at, lanes] = (cosine * real - sine * imag).astype(jnp.bfloat16)
+            wave_ref[colour, at, lanes_imag] = (cosine * imag + sine * real).astype(jnp.bfloat16)
+
+
+def colour_term(colour, vec_ref, wave_ref):
+    return lax.dot_general(
+        vec_ref[colour], wave_ref[colour], (((0,), (0,)), ((), ())), preferred_element_type=jnp.float32
+    )
+
+
+def finish_elemental(term, out_ref):
+    out_ref[:, 0:256] = term[0:256, 0:256] + term[256:512, 256:512]
+    out_ref[:, 256:512] = term[0:256, 256:512] - term[256:512, 0:256]
 
 
 def kernel(
     sink_hbm, source_hbm, per_hbm, mom_ref, snk_t, src_t,
     out_ref,
-    snk_vec, src_vec, wave, cos_ref, sin_ref, acc,
+    snk_vec, src_vec, wave, wave2, cos_ref, sin_ref, acc,
     snk_part, src_part, per, pt, tbuf,
     y_recv, y_sum, z_recv, elem, core_recv, core_sum, x_recv, x_sum, zz_recv, src_elem,
     est, sst, tot,
@@ -104,12 +97,12 @@
         copy.start()
         return copy
 
+    src_loads = [
+        [load(6 + 2 * k + r, source_hbm.at[r, k], src_vec.at[k, :, pl.ds(r * 256, 256)]) for r in range(2)]
+        for k in range(COLOURS)
+    ]
     snk_loads = [
         [load(2 * k + r, sink_hbm.at[r, k], snk_vec.at[k, :, pl.ds(r * 256, 256)]) for r in range(2)]
-        for k in range(COLOURS)
-    ]
-    src_loads = [
-        [load(6 + 2 * k + r, source_hbm.at[r, k], src_vec.at[k, :, pl.ds(r * 256, 256)]) for r in range(2)]
         for k in range(COLOURS)
     ]
     per_loads = [load(12 + s, per_hbm.at[s], per.at[s]) for s in range(4)]
@@ -129,23 +122,46 @@
         for copy in copies:
             copy.start()
 
-    phase_tables(mom_ref, j * (SITES // L), cos_ref, sin_ref)
-    partial_elemental(snk_loads, snk_vec, wave, cos_ref, sin_ref, acc, snk_part)
-    pl.semaphore_wait(barrier, len(peers))
-    sent = []
-
     def block_of(start_row, size):
         return pl.ds(pl.multiple_of(start_row, size), size)
 
+    def loaded(copies):
+        for copy in copies:
+            copy.wait()
+
+    phase_tables(mom_ref, i * (SITES // L), cos_ref, sin_ref)
+    loaded(src_loads[0])
+    wave_of(0, src_vec, wave, cos_ref, sin_ref)
+    loaded(src_loads[1])
+    acc[...] = colour_term(0, src_vec, wave)
+    wave_of(1, src_vec, wave, cos_ref, sin_ref)
+    loaded(src_loads[2])
+    acc[...] += colour_term(1, src_vec, wave)
+    wave_of(2, src_vec, wave, cos_ref, sin_ref)
+    finish_elemental(acc[...] + colour_term(2, src_vec, wave), src_part)
+    pl.semaphore_wait(barrier, len(peers))
+    core_rs = remote(3, src_part.at[block_of(128 * (1 - c), 128)], core_recv, core_peer)
+    core_rs.start()
+
+    phase_tables(mom_ref, j * (SITES // L), cos_ref, sin_ref)
+    for colour in range(COLOURS):
+        loaded(snk_loads[colour])
+    wave_of(0, snk_vec, wave2, cos_ref, sin_ref)
+    acc[...] = colour_term(0, snk_vec, wave2)
+    wave_of(1, snk_vec, wave2, cos_ref, sin_ref)
+    core_rs.wait_recv()
+    core_sum[...] = src_part[block_of(128 * c, 128), :] + core_recv[...]
+    x_rs = [
+        remote(4 + d, core_sum.at[block_of(32 * ((x + d + 1) % 4), 32)], x_recv.at[d], x_peers[d]) for d in range(3)
+    ]
+    start(x_rs)
+    acc[...] += colour_term(1, snk_vec, wave2)
+    wave_of(2, snk_vec, wave2, cos_ref, sin_ref)
+    finish_elemental(acc[...] + colour_term(2, snk_vec, wave2), snk_part)
     y_rs = [
         remote(d, snk_part.at[block_of(64 * ((y + d + 1) % 4), 64)], y_recv.at[d], y_peers[d]) for d in range(3)
     ]
     start(y_rs)
-
-    phase_tables(mom_ref, i * (SITES // L), cos_ref, sin_ref)
-    partial_elemental(src_loads, src_vec, wave, cos_ref, sin_ref, acc, src_part)
-    core_rs = remote(3, src_part.at[block_of(128 * (1 - c), 128)], core_recv, core_peer)
-    core_rs.start()
 
     out_row = lax.broadcasted_iota(jnp.int32, (256, 256), 0)
     in_row = lax.broadcasted_iota(jnp.int32, (256, 256), 1)
@@ -162,19 +178,18 @@
                 for half in range(2):
                     piece = moved[(half * 4 + t) * 32 : (half * 4 + t + 1) * 32, :]
                     for r in range(2):
-                        pt[s, t, pl.ds(blk * 32, 32), pl.ds(r * 256 + half * 128, 128)] = piece[
+                        pt[s, t, r, pl.ds(blk * 32, 32), pl.ds(half * 128, 128)] = piece[
                             :, r * 128 : (r + 1) * 128
                         ]
         return carry
 
-    lax.fori_loop(0, 2, unmix, 0)
-    core_rs.wait_recv()
-    core_sum[...] = src_part[block_of(128 * c, 128), :] + core_recv[...]
-    x_rs = [
-        remote(4 + d, core_sum.at[block_of(32 * ((x + d + 1) % 4), 32)], x_recv.at[d], x_peers[d]) for d in range(3)
-    ]
-    start(x_rs)
-    lax.fori_loop(2, 4, unmix, 0)
+    lax.fori_loop(0, 4, unmix, 0)
+
+    for copy in x_rs:
+        copy.wait_recv()
+    x_sum[...] = (core_sum[block_of(32 * x, 32), :] + x_recv[0]) + (x_recv[1] + x_recv[2])
+    zz = remote(10, x_sum, zz_recv, z_peer)
+    zz.start()
 
     for copy in y_rs:
         copy.wait_recv()
@@ -184,11 +199,13 @@
     ]
     start(z_rs)
 
-    for copy in x_rs:
-        copy.wait_recv()
-    x_sum[...] = (core_sum[block_of(32 * x, 32), :] + x_recv[0]) + (x_recv[1] + x_recv[2])
-    zz = remote(10, x_sum, zz_recv, z_peer)
-    zz.start()
+    zz.wait_recv()
+    src_own = src_elem.at[block_of(128 * c + 32 * x, 32)]
+    src_own[...] = (x_sum[...] + zz_recv[...]).astype(jnp.bfloat16)
+    x_ag = [remote(26 + d, src_own, src_own, x_peers[d]) for d in range(3)]
+    start(x_ag)
+    core_ag = [remote(29, src_own, src_own, core_peer)]
+    start(core_ag)
 
     for copy in z_rs:
         copy.wait_recv()
@@ -200,26 +217,18 @@
     y_ag = [remote(14 + d, own, own, y_peers[d]) for d in range(3)]
     start(y_ag)
 
-    zz.wait_recv()
-    src_own = src_elem.at[block_of(128 * c + 32 * x, 32)]
-    src_own[...] = (x_sum[...] + zz_recv[...]).astype(jnp.bfloat16)
-    x_ag = [remote(26 + d, src_own, src_own, x_peers[d]) for d in range(3)]
-    start(x_ag)
-    core_ag = [remote(29, src_own, src_own, core_peer)]
-    start(core_ag)
-
+    for d in range(3):
+        x_ag[d].wait_recv()
+        came = src_elem.at[block_of(128 * c + 32 * ((x + 3 - d) % 4), 32)]
+        onward = remote(30 + d, came, came, core_peer)
+        onward.start()
+        core_ag.append(onward)
     for d in range(3):
         z_ag[d].wait_recv()
         came = elem.at[block_of(64 * y + 16 * ((zl + 3 - d) % 4), 16)]
         onward = [remote(17 + 3 * d + e, came, came, y_peers[e]) for e in range(3)]
         start(onward)
         y_ag += onward
-    for d in range(3):
-        x_ag[d].wait_recv()
-        came = src_elem.at[block_of(128 * c + 32 * ((x + 3 - d) % 4), 32)]
-        onward = remote(30 + d, came, came, core_peer)
-        onward.start()
-        core_ag.append(onward)
     for copy in core_ag:
         copy.wait_recv()
 
@@ -229,7 +238,8 @@
 
     def right(s, carry):
         for t in range(4):
-            tbuf[s, t] = jnp.dot(pt[s, t], sst[...], preferred_element_type=jnp.float32)
+            rows = jnp.concatenate([pt[s, t, 0], pt[s, t, 1]], axis=1)
+            tbuf[s, t] = jnp.dot(rows, sst[...], preferred_element_type=jnp.float32)
         return carry
 
     lax.fori_loop(0, 4, right, 0)
@@ -250,8 +260,7 @@
         sum_real = jnp.zeros((8, 256), jnp.float32)
         sum_imag = jnp.zeros((8, 256), jnp.float32)
         for t in range(4):
-            lt = jnp.dot(est[:, 0:256], pt[s, t, :, 0:256], preferred_element_type=jnp.float32)
-            lt = lt + jnp.dot(est[:, 256:512], pt[s, t, :, 256:512], preferred_element_type=jnp.float32)
+            lt = jnp.dot(est[...], pt[s, t].reshape(512, 256), preferred_element_type=jnp.float32)
             right_real = tbuf[other, t ^ 2, :, 0:256]
             right_imag = tbuf[other, t ^ 2, :, 256:512]
             left_real = lt[0:256]
@@ -292,13 +301,14 @@
             pltpu.VMEM((COLOURS, SITES, 512), bf16),
             pltpu.VMEM((COLOURS, SITES, 512), bf16),
             pltpu.VMEM((COLOURS, SITES, 512), bf16),
+            pltpu.VMEM((COLOURS, SITES, 512), bf16),
             pltpu.VMEM((SITES, 128), f32),
             pltpu.VMEM((SITES, 128), f32),
             pltpu.VMEM((512, 512), f32),
             pltpu.VMEM((256, 512), f32),
             pltpu.VMEM((256, 512), f32),
             pltpu.VMEM((4, 2, 2048, 128), bf16),
-            pltpu.VMEM((4, 4, 256, 512), bf16),
+            pltpu.VMEM((4, 4, 2, 256, 256), bf16),
             pltpu.VMEM((4, 4, 256, 512), f32),
             pltpu.VMEM((3, 64, 512), f32),
             pltpu.VMEM((64, 512), f32),

time: 46.7 us -> 41.9 us (0.90)
  the two profiles are of different devices: /device:TPU:1 before, /device:TPU:4 now
where the time goes in v2:
time: 41.9 us; the launch traced here: 41.8 us
  Pallas kernels  39.3 us (94%)
  between operations  1.3 us (3%)
  local copies, waits for them, and re-layouts  1.19 us (3%)
    pallas_call x1, Pallas kernels, per_device(): pl.pallas_call(kernel, out_shape=jax.ShapeDtypeStruct((1, 2), f32), in_sp...  39.3 us
    unnamed x1, local copies, waits for them, and re-layouts  1.19 us

profile of v2, /device:TPU:4, one launch (start us, length us, event | category | flops | bytes accessed | tf_op | source)
XLA Modules:
  0.0 41.8 jit_solution(38414506008021405)
XLA Ops:
  1.3 39.3 %shard_map.64 = f32[1,2]{1,0:T(1,128)} custom-call(bf16[2,3,864,256]{3,2,1,0:T(8,128)(2,1)} %bitcast.13, bf16[2,3,864,256]{3,2,1,0:T(8,128)(2,1)} %bitcast.14, bf16[4,2,2048,128]{3,2,1,0:T(8,128)(2,1)} %bitcast.12, s32[1,3]{1,0:T(1,128)} %mom_ref.1, s32[1]{0:T(128)S(6)} %copy.9.snk_t, s32[1]{0:T(128)S(6)} %copy.10.src_t), custom_call_target="tpu_custom_call" | custom-call | tf_op jit(solution)/shard_map/pallas_call | solution.py:295
  40.6 1.2 %copy.11 = f32[1,2,1,1]{1,3,2,0:T(1,128)} copy(f32[1,2,1,1]{1,3,2,0:T(1,128)} %bitcast.15) | data formatting | bytes 16

commit v3 on v2

--- a/solution.py
+++ b/solution.py
@@ -47,25 +47,31 @@
         sin_ref[q * L : (q + 1) * L, :] = sq * cos_z + cq * sin_z
 
 
-def wave_of(colour, vec_ref, wave_ref, cos_ref, sin_ref):
-    rows = 48
-    for step in range(SITES // rows):
-        at = pl.ds(step * rows, rows)
-        cosine = cos_ref[at, :]
-        sine = sin_ref[at, :]
+CHUNKS = ((0, 512), (512, 1024), (1536, 1056))
+
+
+def wave_of(chunk, vec_ref, wave_ref, cos_ref, sin_ref):
+    first, count = CHUNKS[chunk]
+    row = first
+    while row < first + count:
+        site = row % SITES
+        rows = min(48, first + count - row, SITES - site)
+        at = pl.ds(row, rows)
+        cosine = cos_ref[pl.ds(site, rows), :]
+        sine = sin_ref[pl.ds(site, rows), :]
         for half in range(2):
             lanes = pl.ds(half * 128, 128)
             lanes_imag = pl.ds(256 + half * 128, 128)
-            real = vec_ref[colour, at, lanes].astype(jnp.float32)
-            imag = vec_ref[colour, at, lanes_imag].astype(jnp.float32)
-            wave_ref[colour, at, lanes] = (cosine * real - sine * imag).astype(jnp.bfloat16)
-            wave_ref[colour, at, lanes_imag] = (cosine * imag + sine * real).astype(jnp.bfloat16)
-
-
-def colour_term(colour, vec_ref, wave_ref):
-    return lax.dot_general(
-        vec_ref[colour], wave_ref[colour], (((0,), (0,)), ((), ())), preferred_element_type=jnp.float32
-    )
+            real = vec_ref[at, lanes].astype(jnp.float32)
+            imag = vec_ref[at, lanes_imag].astype(jnp.float32)
+            wave_ref[at, lanes] = (cosine * real - sine * imag).astype(jnp.bfloat16)
+            wave_ref[at, lanes_imag] = (cosine * imag + sine * real).astype(jnp.bfloat16)
+        row += rows
+
+
+def colour_term(chunk, vec_ref, wave_ref):
+    at = pl.ds(*CHUNKS[chunk])
+    return lax.dot_general(vec_ref[at, :], wave_ref[at, :], (((0,), (0,)), ((), ())), preferred_element_type=jnp.float32)
 
 
 def finish_elemental(term, out_ref):
@@ -78,7 +84,7 @@
     out_ref,
     snk_vec, src_vec, wave, wave2, cos_ref, sin_ref, acc,
     snk_part, src_part, per, pt, tbuf,
-    y_recv, y_sum, z_recv, elem, core_recv, core_sum, x_recv, x_sum, zz_recv, src_elem,
+    y_recv, y_far, y_far_recv, y_sum, z_recv, elem, core_recv, core_sum, x_recv, x_sum, zz_recv, src_elem,
     est, sst, tot,
     load_sem, send_sem, recv_sem,
 ):
@@ -93,19 +99,20 @@
     zl_peers = [(i, 4 * y + (zl + d) % 4) for d in (1, 2, 3)]
 
     def load(n, src, dst):
-        copy = pltpu.make_async_copy(src, dst, load_sem.at[n])
-        copy.start()
-        return copy
+        return pltpu.make_async_copy(src, dst, load_sem.at[n])
 
     src_loads = [
-        [load(6 + 2 * k + r, source_hbm.at[r, k], src_vec.at[k, :, pl.ds(r * 256, 256)]) for r in range(2)]
+        [load(6 + 2 * k + r, source_hbm.at[r, k], src_vec.at[pl.ds(k * SITES, SITES), pl.ds(r * 256, 256)]) for r in range(2)]
         for k in range(COLOURS)
     ]
     snk_loads = [
-        [load(2 * k + r, sink_hbm.at[r, k], snk_vec.at[k, :, pl.ds(r * 256, 256)]) for r in range(2)]
+        [load(2 * k + r, sink_hbm.at[r, k], snk_vec.at[pl.ds(k * SITES, SITES), pl.ds(r * 256, 256)]) for r in range(2)]
         for k in range(COLOURS)
     ]
     per_loads = [load(12 + s, per_hbm.at[s], per.at[s]) for s in range(4)]
+    for copies in src_loads:
+        for copy in copies:
+            copy.start()
 
     barrier = pltpu.get_barrier_semaphore()
     peers = [core_peer, z_peer] + x_peers + y_peers + zl_peers
@@ -133,6 +140,8 @@
     loaded(src_loads[0])
     wave_of(0, src_vec, wave, cos_ref, sin_ref)
     loaded(src_loads[1])
+    for copies in snk_loads:
+        start(copies)
     acc[...] = colour_term(0, src_vec, wave)
     wave_of(1, src_vec, wave, cos_ref, sin_ref)
     loaded(src_loads[2])
@@ -142,6 +151,8 @@
     pl.semaphore_wait(barrier, len(peers))
     core_rs = remote(3, src_part.at[block_of(128 * (1 - c), 128)], core_recv, core_peer)
     core_rs.start()
+
+    start(per_loads)
 
     phase_tables(mom_ref, j * (SITES // L), cos_ref, sin_ref)
     for colour in range(COLOURS):
@@ -158,8 +169,11 @@
     acc[...] += colour_term(1, snk_vec, wave2)
     wave_of(2, snk_vec, wave2, cos_ref, sin_ref)
     finish_elemental(acc[...] + colour_term(2, snk_vec, wave2), snk_part)
+    y_far[...] = snk_part[block_of(64 * ((y + 2) % 4), 64), :].astype(jnp.bfloat16)
     y_rs = [
-        remote(d, snk_part.at[block_of(64 * ((y + d + 1) % 4), 64)], y_recv.at[d], y_peers[d]) for d in range(3)
+        remote(0, snk_part.at[block_of(64 * ((y + 1) % 4), 64)], y_recv.at[0], y_peers[0]),
+        remote(2, snk_part.at[block_of(64 * ((y + 3) % 4), 64)], y_recv.at[1], y_peers[2]),
+        remote(1, y_far, y_far_recv, y_peers[1]),
     ]
     start(y_rs)
 
@@ -178,7 +192,7 @@
                 for half in range(2):
                     piece = moved[(half * 4 + t) * 32 : (half * 4 + t + 1) * 32, :]
                     for r in range(2):
-                        pt[s, t, r, pl.ds(blk * 32, 32), pl.ds(half * 128, 128)] = piece[
+                        pt[s, r, t, pl.ds(blk * 32, 32), pl.ds(half * 128, 128)] = piece[
                             :, r * 128 : (r + 1) * 128
                         ]
         return carry
@@ -193,7 +207,9 @@
 
     for copy in y_rs:
         copy.wait_recv()
-    y_sum[...] = (snk_part[block_of(64 * y, 64), :] + y_recv[0]) + (y_recv[1] + y_recv[2])
+    y_sum[...] = (snk_part[block_of(64 * y, 64), :] + y_recv[0]) + (
+        y_recv[1] + y_far_recv[...].astype(jnp.float32)
+    )
     z_rs = [
         remote(7 + d, y_sum.at[block_of(16 * ((zl + d + 1) % 4), 16)], z_recv.at[d], zl_peers[d]) for d in range(3)
     ]
@@ -237,12 +253,11 @@
     sst[256:512, 256:512] = src_elem[:, 0:256]
 
     def right(s, carry):
-        for t in range(4):
-            rows = jnp.concatenate([pt[s, t, 0], pt[s, t, 1]], axis=1)
-            tbuf[s, t] = jnp.dot(rows, sst[...], preferred_element_type=jnp.float32)
+        rows = jnp.concatenate([pt[s, 0].reshape(1024, 256), pt[s, 1].reshape(1024, 256)], axis=1)
+        tbuf[s] = jnp.dot(rows, sst[...], preferred_element_type=jnp.float32).reshape(4, 256, 512)
         return carry
 
-    lax.fori_loop(0, 4, right, 0)
+    lax.fori_loop(0, 4, right, 0, unroll=True)
 
     for copy in y_ag:
         copy.wait_recv()
@@ -260,7 +275,7 @@
         sum_real = jnp.zeros((8, 256), jnp.float32)
         sum_imag = jnp.zeros((8, 256), jnp.float32)
         for t in range(4):
-            lt = jnp.dot(est[...], pt[s, t].reshape(512, 256), preferred_element_type=jnp.float32)
+            lt = jnp.dot(est[...], jnp.concatenate([pt[s, 0, t], pt[s, 1, t]], axis=0), preferred_element_type=jnp.float32)
             right_real = tbuf[other, t ^ 2, :, 0:256]
             right_imag = tbuf[other, t ^ 2, :, 256:512]
             left_real = lt[0:256]
@@ -276,7 +291,7 @@
         tot[1] += sign * sum_imag
         return carry
 
-    lax.fori_loop(0, 4, left, 0)
+    lax.fori_loop(0, 4, left, 0, unroll=True)
     keep = jnp.where(snk_t[0] >= src_t[0], 1.0, 0.0)
     out_ref[0, 0] = jnp.sum(tot[0]) * keep
     out_ref[0, 1] = jnp.sum(tot[1]) * keep
@@ -298,19 +313,21 @@
         in_specs=[hbm, hbm, hbm, smem, smem, smem],
         out_specs=smem,
         scratch_shapes=[
-            pltpu.VMEM((COLOURS, SITES, 512), bf16),
-            pltpu.VMEM((COLOURS, SITES, 512), bf16),
-            pltpu.VMEM((COLOURS, SITES, 512), bf16),
-            pltpu.VMEM((COLOURS, SITES, 512), bf16),
+            pltpu.VMEM((COLOURS * SITES, 512), bf16),
+            pltpu.VMEM((COLOURS * SITES, 512), bf16),
+            pltpu.VMEM((COLOURS * SITES, 512), bf16),
+            pltpu.VMEM((COLOURS * SITES, 512), bf16),
             pltpu.VMEM((SITES, 128), f32),
             pltpu.VMEM((SITES, 128), f32),
             pltpu.VMEM((512, 512), f32),
             pltpu.VMEM((256, 512), f32),
             pltpu.VMEM((256, 512), f32),
             pltpu.VMEM((4, 2, 2048, 128), bf16),
-            pltpu.VMEM((4, 4, 2, 256, 256), bf16),
+            pltpu.VMEM((4, 2, 4, 256, 256), bf16),
             pltpu.VMEM((4, 4, 256, 512), f32),
-            pltpu.VMEM((3, 64, 512), f32),
+            pltpu.VMEM((2, 64, 512), f32),
+            pltpu.VMEM((64, 512), bf16),
+            pltpu.VMEM((64, 512), bf16),
             pltpu.VMEM((64, 512), f32),
             pltpu.VMEM((3, 16, 512), f32),
             pltpu.VMEM((256, 512), bf16),

time: 41.9 us -> 40.8 us (0.974)
  Pallas kernels: 39.3 us -> 37.9 us
    pallas_call x1, Pallas kernels: 39.3 us -> 37.9 us  [per_device(): pl.pallas_call(kernel, out_shape=jax.ShapeDtypeStruct((1, 2), f32), in_sp...]
where the time goes in v3:
time: 40.8 us; the launch traced here: 40.4 us
  Pallas kernels  37.9 us (93%)
  between operations  1.3 us (3%)
  local copies, waits for them, and re-layouts  1.19 us (3%)
    pallas_call x1, Pallas kernels, per_device(): pl.pallas_call(kernel, out_shape=jax.ShapeDtypeStruct((1, 2), f32), in_sp...  37.9 us
    unnamed x1, local copies, waits for them, and re-layouts  1.19 us

profile of v3, /device:TPU:4, one launch (start us, length us, event | category | flops | bytes accessed | tf_op | source)
XLA Modules:
  0.0 40.4 jit_solution(15287578135854989170)
XLA Ops:
  1.3 37.9 %shard_map.64 = f32[1,2]{1,0:T(1,128)} custom-call(bf16[2,3,864,256]{3,2,1,0:T(8,128)(2,1)} %bitcast.13, bf16[2,3,864,256]{3,2,1,0:T(8,128)(2,1)} %bitcast.14, bf16[4,2,2048,128]{3,2,1,0:T(8,128)(2,1)} %bitcast.12, s32[1,3]{1,0:T(1,128)} %mom_ref.1, s32[1]{0:T(128)S(6)} %copy.9.snk_t, s32[1]{0:T(128)S(6)} %copy.10.src_t), custom_call_target="tpu_custom_call" | custom-call | tf_op jit(solution)/shard_map/pallas_call | solution.py:310
  39.2 1.2 %copy.11 = f32[1,2,1,1]{1,3,2,0:T(1,128)} copy(f32[1,2,1,1]{1,3,2,0:T(1,128)} %bitcast.15) | data formatting | bytes 16

commit v4 on v3

--- a/solution.py
+++ b/solution.py
@@ -47,7 +47,7 @@
         sin_ref[q * L : (q + 1) * L, :] = sq * cos_z + cq * sin_z
 
 
-CHUNKS = ((0, 512), (512, 1024), (1536, 1056))
+CHUNKS = ((0, 256), (256, 1024), (1280, 1312))
 
 
 def wave_of(chunk, vec_ref, wave_ref, cos_ref, sin_ref):
@@ -84,7 +84,7 @@
     out_ref,
     snk_vec, src_vec, wave, wave2, cos_ref, sin_ref, acc,
     snk_part, src_part, per, pt, tbuf,
-    y_recv, y_far, y_far_recv, y_sum, z_recv, elem, core_recv, core_sum, x_recv, x_sum, zz_recv, src_elem,
+    y_recv, y_sum, z_recv, elem, core_recv, core_sum, x_recv, x_sum, zz_recv, src_elem,
     est, sst, tot,
     load_sem, send_sem, recv_sem,
 ):
@@ -160,20 +160,17 @@
     wave_of(0, snk_vec, wave2, cos_ref, sin_ref)
     acc[...] = colour_term(0, snk_vec, wave2)
     wave_of(1, snk_vec, wave2, cos_ref, sin_ref)
+    acc[...] += colour_term(1, snk_vec, wave2)
+    wave_of(2, snk_vec, wave2, cos_ref, sin_ref)
     core_rs.wait_recv()
     core_sum[...] = src_part[block_of(128 * c, 128), :] + core_recv[...]
     x_rs = [
         remote(4 + d, core_sum.at[block_of(32 * ((x + d + 1) % 4), 32)], x_recv.at[d], x_peers[d]) for d in range(3)
     ]
     start(x_rs)
-    acc[...] += colour_term(1, snk_vec, wave2)
-    wave_of(2, snk_vec, wave2, cos_ref, sin_ref)
     finish_elemental(acc[...] + colour_term(2, snk_vec, wave2), snk_part)
-    y_far[...] = snk_part[block_of(64 * ((y + 2) % 4), 64), :].astype(jnp.bfloat16)
     y_rs = [
-        remote(0, snk_part.at[block_of(64 * ((y + 1) % 4), 64)], y_recv.at[0], y_peers[0]),
-        remote(2, snk_part.at[block_of(64 * ((y + 3) % 4), 64)], y_recv.at[1], y_peers[2]),
-        remote(1, y_far, y_far_recv, y_peers[1]),
+        remote(d, snk_part.at[block_of(64 * ((y + d + 1) % 4), 64)], y_recv.at[d], y_peers[d]) for d in range(3)
     ]
     start(y_rs)
 
@@ -207,9 +204,7 @@
 
     for copy in y_rs:
         copy.wait_recv()
-    y_sum[...] = (snk_part[block_of(64 * y, 64), :] + y_recv[0]) + (
-        y_recv[1] + y_far_recv[...].astype(jnp.float32)
-    )
+    y_sum[...] = (snk_part[block_of(64 * y, 64), :] + y_recv[0]) + (y_recv[1] + y_recv[2])
     z_rs = [
         remote(7 + d, y_sum.at[block_of(16 * ((zl + d + 1) % 4), 16)], z_recv.at[d], zl_peers[d]) for d in range(3)
     ]
@@ -325,9 +320,7 @@
             pltpu.VMEM((4, 2, 2048, 128), bf16),
             pltpu.VMEM((4, 2, 4, 256, 256), bf16),
             pltpu.VMEM((4, 4, 256, 512), f32),
-            pltpu.VMEM((2, 64, 512), f32),
-            pltpu.VMEM((64, 512), bf16),
-            pltpu.VMEM((64, 512), bf16),
+            pltpu.VMEM((3, 64, 512), f32),
             pltpu.VMEM((64, 512), f32),
             pltpu.VMEM((3, 16, 512), f32),
             pltpu.VMEM((256, 512), bf16),

time: 40.8 us -> 40.8 us (level)
  no operation moved by 1% of the time
where the time goes in v4:
time: 40.8 us; the launch traced here: 40.7 us
  Pallas kernels  38.2 us (94%)
  between operations  1.3 us (3%)
  local copies, waits for them, and re-layouts  1.19 us (3%)
    pallas_call x1, Pallas kernels, per_device(): pl.pallas_call(kernel, out_shape=jax.ShapeDtypeStruct((1, 2), f32), in_sp...  38.2 us
    unnamed x1, local copies, waits for them, and re-layouts  1.19 us

profile of v4, /device:TPU:4, one launch (start us, length us, event | category | flops | bytes accessed | tf_op | source)
XLA Modules:
  0.0 40.7 jit_solution(3604478852484482188)
XLA Ops:
  1.3 38.2 %shard_map.64 = f32[1,2]{1,0:T(1,128)} custom-call(bf16[2,3,864,256]{3,2,1,0:T(8,128)(2,1)} %bitcast.13, bf16[2,3,864,256]{3,2,1,0:T(8,128)(2,1)} %bitcast.14, bf16[4,2,2048,128]{3,2,1,0:T(8,128)(2,1)} %bitcast.12, s32[1,3]{1,0:T(1,128)} %mom_ref.1, s32[1]{0:T(128)S(6)} %copy.9.snk_t, s32[1]{0:T(128)S(6)} %copy.10.src_t), custom_call_target="tpu_custom_call" | custom-call | tf_op jit(solution)/shard_map/pallas_call | solution.py:305
  39.5 1.2 %copy.11 = f32[1,2,1,1]{1,3,2,0:T(1,128)} copy(f32[1,2,1,1]{1,3,2,0:T(1,128)} %bitcast.15) | data formatting | bytes 16

commit v5 on v4

--- a/solution.py
+++ b/solution.py
@@ -229,17 +229,17 @@
     start(y_ag)
 
     for d in range(3):
+        z_ag[d].wait_recv()
+        came = elem.at[block_of(64 * y + 16 * ((zl + 3 - d) % 4), 16)]
+        onward = [remote(17 + 3 * d + e, came, came, y_peers[e]) for e in range(3)]
+        start(onward)
+        y_ag += onward
+    for d in range(3):
         x_ag[d].wait_recv()
         came = src_elem.at[block_of(128 * c + 32 * ((x + 3 - d) % 4), 32)]
         onward = remote(30 + d, came, came, core_peer)
         onward.start()
         core_ag.append(onward)
-    for d in range(3):
-        z_ag[d].wait_recv()
-        came = elem.at[block_of(64 * y + 16 * ((zl + 3 - d) % 4), 16)]
-        onward = [remote(17 + 3 * d + e, came, came, y_peers[e]) for e in range(3)]
-        start(onward)
-        y_ag += onward
     for copy in core_ag:
         copy.wait_recv()
 

time: 40.8 us -> 41.4 us (1.015); the launches traced: 40.7 us -> 40.7 us
  no operation moved by 1% of the time
where the time goes in v5:
time: 41.4 us; the launch traced here: 40.7 us
  Pallas kernels  38.2 us (92%)
  between operations  1.3 us (3%)
  local copies, waits for them, and re-layouts  1.19 us (3%)
    pallas_call x1, Pallas kernels, per_device(): pl.pallas_call(kernel, out_shape=jax.ShapeDtypeStruct((1, 2), f32), in_sp...  38.2 us
    unnamed x1, local copies, waits for them, and re-layouts  1.19 us

profile of v5, /device:TPU:4, one launch (start us, length us, event | category | flops | bytes accessed | tf_op | source)
XLA Modules:
  0.0 40.7 jit_solution(179444744857618930)
XLA Ops:
  1.3 38.2 %shard_map.64 = f32[1,2]{1,0:T(1,128)} custom-call(bf16[2,3,864,256]{3,2,1,0:T(8,128)(2,1)} %bitcast.13, bf16[2,3,864,256]{3,2,1,0:T(8,128)(2,1)} %bitcast.14, bf16[4,2,2048,128]{3,2,1,0:T(8,128)(2,1)} %bitcast.12, s32[1,3]{1,0:T(1,128)} %mom_ref.1, s32[1]{0:T(128)S(6)} %copy.9.snk_t, s32[1]{0:T(128)S(6)} %copy.10.src_t), custom_call_target="tpu_custom_call" | custom-call | tf_op jit(solution)/shard_map/pallas_call | solution.py:305
  39.5 1.2 %copy.11 = f32[1,2,1,1]{1,3,2,0:T(1,128)} copy(f32[1,2,1,1]{1,3,2,0:T(1,128)} %bitcast.15) | data formatting | bytes 16
